TPU v7x, 32 devices: a whole 2x2x4 slice. The times are simulated.
32 devices in a mesh: seq: 8 (over z, core), tp: 4 (over y, x).
Axes of the slice: x: 2, y: 2, z: 4, core: 2. Of those that a mesh axis runs over, the one named last changes fastest.
Arguments:
- tokens: bfloat16 [1024, 8192], P('seq'), may hold values from -6 to 6
- conv_weight: float32 [4, 8192], replicated, may hold values from -3 to 3
- norm_gain: float32 [8192], replicated, may hold values from 0.25 to 1.75
- gate_weight: bfloat16 [8192, 14336], P('seq', 'tp'), may hold values from -0.0625 to 0.0625
- up_weight: bfloat16 [8192, 14336], P('seq', 'tp'), may hold values from -0.0625 to 0.0625
- down_weight: bfloat16 [14336, 8192], P('tp', 'seq'), may hold values from -0.046875 to 0.046875
Outputs:
- mixed_out: bfloat16 [1024, 8192], P(('seq', 'tp'))
All inputs are finite; a program needn't handle non-finite values.
Results may differ from a plain program's by a relative error of at most 0.03.
Values may be sent and summed in bfloat16 or wider, within the bound.
A program may use at most 128 MiB of HBM per device.

v0:
```python
import jax
import jax.numpy as jnp
from jax import lax
from jax.sharding import PartitionSpec as P


def from_behind(shard, axis, by):
    peers = lax.axis_size(axis)
    pairs = [(i, i + by) for i in range(peers) if 0 <= i + by < peers]
    return lax.ppermute(shard, axis, pairs)


def swiglu(both_sums, half_cols):
    return (jax.nn.silu(both_sums[:, :half_cols]) * both_sums[:, half_cols:]).astype(jnp.bfloat16)


def shards(tokens, conv_weight, norm_gain, gate_weight, up_weight, down_weight):
    tok_rows = tokens.shape[0]
    taps_count = conv_weight.shape[0]
    seq_count = lax.axis_size("seq")
    edge_rows = from_behind(tokens[tok_rows - (taps_count - 1) :], "seq", 1)
    extended = jnp.concatenate([edge_rows, tokens], 0).astype(jnp.float32)
    conv_out = jnp.zeros(tokens.shape, jnp.float32)
    for tap_index in range(taps_count):
        begin = taps_count - 1 - tap_index
        conv_out = conv_out + conv_weight[tap_index][None, :] * extended[begin : begin + tok_rows]
    scale_rms = lax.rsqrt(jnp.mean(conv_out * conv_out, axis=-1, keepdims=True) + 1e-05)
    normed = (conv_out * scale_rms * norm_gain[None, :]).astype(jnp.bfloat16)
    all_rows = lax.all_to_all(normed, "seq", split_axis=1, concat_axis=0, tiled=True)
    half_cols = gate_weight.shape[1]
    w_both = jnp.concatenate([gate_weight, up_weight], 1)
    gate_share = lax.psum_scatter(
        jnp.dot(all_rows, w_both, preferred_element_type=jnp.float32).astype(jnp.bfloat16),
        "seq",
        scatter_dimension=0,
        tiled=True,
    ).astype(jnp.float32)
    hidden = swiglu(gate_share, half_cols)
    out_terms = jnp.dot(
        lax.all_gather(hidden, "seq", axis=0, tiled=True),
        down_weight,
        preferred_element_type=jnp.float32,
    )
    col_width = out_terms.shape[1]
    out_terms = out_terms.reshape(seq_count, tok_rows, col_width)
    summed = lax.psum_scatter(out_terms.astype(jnp.bfloat16), "tp", scatter_dimension=1, tiled=True)
    mixed_out = lax.all_to_all(summed, "seq", split_axis=0, concat_axis=2, tiled=True)
    return mixed_out.reshape(mixed_out.shape[1], mixed_out.shape[2])


def solution(mesh):
    in_specs = (P("seq", None), P(), P(), P("seq", "tp"), P("seq", "tp"), P("tp", "seq"))
    out_specs = P(("seq", "tp"), None)
    return jax.shard_map(shards, mesh=mesh, in_specs=in_specs, out_specs=out_specs, check_vma=False)
```

profile of v0, /device:TPU:0, one launch (start us, length us, event | category | flops | bytes accessed | tf_op | source)
XLA Modules:
  0.0 409.3 jit_solution(17760382771565718284)
XLA Ops:
  6.5 0.9 slice.34
  7.5 2.4 collective-permute-start
  9.9 1.3 fusion.13
  11.2 3.2 copy.14
  14.4 1.9 copy.13
  16.3 3.1 maximum_convert_fusion
  19.4 8.7 %multiply_reduce_fusion = (f32[128]{0:T(128)S(1)}, f32[128,8192]{0,1:T(8,128)S(1)}) fusion(f32[131,8192]{0,1:T(8,128)S(1)} %maximum_convert_fusion, f32[8192]{0:T(1024)S(1)} %bitcast.26, f32[8192]{0:T(1024)S(1)} %bitcast.27, f32[8192]{0:T(1024)S(1)} %bitcast.25, f32[8192]{0:T(1024)S(1)} %bitcast.24), kind=kLoop, calls=%fused_computation.14 | loop fusion | flops 9437056 | bytes 21103104 | tf_op jit(solution)/shard_map/reduce_sum | solution.py:27
  28.2 3.5 multiply_convert_fusion
  31.6 55.0 %all_to_all.34 = bf16[128,8,1024]{0,2,1:T(8,128)(2,1)S(1)} all-to-all(bf16[128,8,1024]{0,2,1:T(8,128)(2,1)S(1)} %bitcast.19), channel_id=1, replica_groups=mesh['seq'=8,'tp'=4] {'seq'}, dimensions={1} | all-to-all | bytes 4194304 | tf_op jit(solution)/shard_map/all_to_all | solution.py:29
  86.6 2.6 copy.15
  89.2 22.3 %fusion.4 = bf16[1024,7168]{1,0:T(8,128)(2,1)} fusion(bf16[1024,1024]{1,0:T(8,128)(2,1)} %bitcast.22, bf16[1024,3584]{1,0:T(8,128)(2,1)} %param.10, bf16[1024,3584]{1,0:T(8,128)(2,1)} %param.9), kind=kOutput, calls=%fused_computation.4 | convolution fusion | flops 15069085696 | bytes 31457280 | tf_op jit(solution)/shard_map/dot_general | solution.py:33
  111.6 0.0 reduce-scatter.3.cloned.1.call-update
  111.6 0.0 all-gather.2.cloned.1.call-start
  111.6 148.0 %reduce-scatter.3.cloned.1.call-done = bf16[128,7168]{1,0:T(8,128)(2,1)} async-done(((bf16[1024,7168]{1,0:T(8,128)(2,1)}), bf16[128,7168]{1,0:T(8,128)(2,1)}) %reduce-scatter.3.cloned.1.call-update) | async-done | bytes 1835024 | tf_op jit(solution)/shard_map/reduce_scatter | solution.py:32
  259.6 1.9 convert_element_type.24
  261.5 1.4 fusion.10
  262.9 0.0 all-gather.2.cloned.1.call-update
  263.0 0.0 reduce-scatter.5.cloned.1.call-start
  263.0 71.9 %all-gather.2.cloned.1.call-done = bf16[1024,3584]{1,0:T(8,128)(2,1)} async-done(((bf16[128,3584]{1,0:T(8,128)(2,1)}), bf16[1024,3584]{1,0:T(8,128)(2,1)}) %all-gather.2.cloned.1.call-update) | async-done | bytes 7340048 | tf_op jit(solution)/shard_map/all_gather | solution.py:40
  334.9 13.2 %convolution_convert_fusion = bf16[1024,1024]{1,0:T(8,128)(2,1)} fusion(bf16[1024,3584]{1,0:T(8,128)(2,1)} %all-gather.2.cloned.1.call-done, bf16[3584,1024]{1,0:T(8,128)(2,1)} %param.11), kind=kOutput, calls=%fused_computation.15 | convolution fusion | flops 7517241344 | bytes 16777216 | tf_op jit(solution)/shard_map/dot_general | solution.py:39
  348.1 0.0 reduce-scatter.5.cloned.1.call-update
  348.1 33.9 %reduce-scatter.5.cloned.1.call-done = bf16[8,32,1024]{2,1,0:T(8,128)(2,1)} async-done(((bf16[8,128,1024]{2,1,0:T(8,128)(2,1)}), bf16[8,32,1024]{2,1,0:T(8,128)(2,1)}) %reduce-scatter.5.cloned.1.call-update) | async-done | bytes 524304 | tf_op jit(solution)/shard_map/reduce_scatter | solution.py:46
  382.1 19.9 %all_to_all.35 = bf16[8,32,1024]{2,1,0:T(8,128)(2,1)S(1)} all-to-all(bf16[8,32,1024]{2,1,0:T(8,128)(2,1)} %reduce-scatter.5.cloned.1.call-done), channel_id=1, replica_groups=mesh['seq'=8,'tp'=4] {'seq'}, dimensions={0} | all-to-all | bytes 1048576 | tf_op jit(solution)/shard_map/all_to_all | solution.py:47
  402.0 0.8 copy.17
  (5 shorter events, 0.0 us)
Async XLA Ops:
  6.5 253.1 %reduce-scatter.3.cloned.1.call-start = ((), (), s32[]{:S(2)}) async-start(), calls=%async_computation.4 | async-start | bytes 16515072 | tf_op jit(solution)/shard_map/reduce_scatter | solution.py:32
  7.5 6.9 %collective-permute-start = (bf16[3,8192]{1,0:T(4,128)(2,1)S(1)}, bf16[3,8192]{1,0:T(4,128)(2,1)S(1)}, u32[]{:S(2)}, u32[]{:S(2)}) collective-permute-start(bf16[3,8192]{1,0:T(4,128)(2,1)S(1)} %slice.34), channel_id=1, source_target_pairs={{0,4},{4,8},{8,12},{12,16},{16,20},{20,24},{24,28},{1,5},{5,9},{9,... | collective-permute-start | bytes 147464 | tf_op jit(solution)/shard_map/ppermute | solution.py:10
  19.4 8.8 %copy-start = (f32[8192]{0:T(1024)S(1)}, f32[8192]{0:T(1024)}, u32[]{:S(2)}) copy-start(f32[8192]{0:T(1024)} %param.8) | copy-start | bytes 98308
  111.6 223.3 %all-gather.2.cloned.1.call-start = ((), (), s32[]{:S(2)}) async-start(), calls=%async_computation.5 | async-start | bytes 8257536 | tf_op jit(solution)/shard_map/all_gather | solution.py:40
  263.0 119.1 %reduce-scatter.5.cloned.1.call-start = ((), (), s32[]{:S(2)}) async-start(), calls=%async_computation.6 | async-start | bytes 2621440 | tf_op jit(solution)/shard_map/reduce_scatter | solution.py:46
Sparse Core Ops, SparseCore 0:
  111.7 147.8 reduce-scatter.2
  263.1 71.8 all-gather.1
  348.3 33.7 reduce-scatter.4
where the time goes:
time: 410 us; the launch traced here: 409 us
  waiting for transfers between devices  254 us (62%)
  blocking collectives  74.9 us (18%)
  matrix products  35.5 us (9%)
  other arithmetic  18.6 us (5%)
  between operations  13.2 us (3%)
  local copies, waits for them, and re-layouts  10.8 us (3%)
    reduce_scatter x1, waiting for transfers between devices, shards(): lax.psum_scatter(jnp.dot(all_rows, w_both, preferred_element_type=jnp.flo...  148 us
    all_gather x1, waiting for transfers between devices, shards(): lax.all_gather(hidden, 'seq', axis=0, tiled=True)  71.9 us
    all_to_all x1, blocking collectives, shards(): lax.all_to_all(normed, 'seq', split_axis=1, concat_axis=0, tiled=True)  55 us
    reduce_scatter x1, waiting for transfers between devices, shards(): lax.psum_scatter(out_terms.astype(jnp.bfloat16), 'tp', scatter_dimension=...  33.9 us
    dot_general x1, matrix products, shards(): jnp.dot(all_rows, w_both, preferred_element_type=jnp.float32)  22.3 us
    all_to_all x1, blocking collectives, shards(): lax.all_to_all(summed, 'seq', split_axis=0, concat_axis=2, tiled=True)  19.9 us
    dot_general x1, matrix products, shards(): jnp.dot(lax.all_gather(hidden, 'seq', axis=0, tiled=True), down_weight, p...  13.2 us
    reduce_sum x1, other arithmetic, shards(): jnp.mean(conv_out * conv_out, axis=-1, keepdims=True) + 1e-05  8.75 us
  transfers between devices with their start and end apart: 4, of which 3 were waited for; matrix products, arithmetic and copies ran while one was open for 1% of the time, Pallas kernels for 0%

commit v1 on v0

--- a/solution.py
+++ b/solution.py
@@ -26,7 +26,10 @@
         conv_out = conv_out + conv_weight[tap_index][None, :] * extended[begin : begin + tok_rows]
     scale_rms = lax.rsqrt(jnp.mean(conv_out * conv_out, axis=-1, keepdims=True) + 1e-05)
     normed = (conv_out * scale_rms * norm_gain[None, :]).astype(jnp.bfloat16)
-    all_rows = lax.all_to_all(normed, "seq", split_axis=1, concat_axis=0, tiled=True)
+    all_rows = jnp.concatenate(
+        lax.all_to_all(jnp.stack(jnp.split(normed, lax.axis_size("seq"), axis=1)), "seq", 0, 0),
+        axis=0,
+    )
     half_cols = gate_weight.shape[1]
     w_both = jnp.concatenate([gate_weight, up_weight], 1)
     gate_share = lax.psum_scatter(

time: 410 us -> 394 us (0.961)
  other arithmetic: 18.6 us -> 8.2 us
  local copies, waits for them, and re-layouts: 10.8 us -> 3.22 us
    reduce_sum x1, other arithmetic: 8.75 us -> 2.21 us  [shards(): jnp.mean(conv_out * conv_out, axis=-1, keepdims=True) + 1e-05]
  transfers between devices with their start and end apart: 4 -> 4, of which waited for: 3 -> 3; matrix products, arithmetic and copies ran while one was open for 1% -> 0% of each run, Pallas kernels for 0% -> 0%
where the time goes in v1:
time: 394 us; the launch traced here: 393 us
  waiting for transfers between devices  254 us (64%)
  blocking collectives  77.3 us (20%)
  matrix products  34.9 us (9%)
  between operations  13.3 us (3%)
  other arithmetic  8.2 us (2%)
    reduce_scatter x1, waiting for transfers between devices, shards(): lax.psum_scatter(jnp.dot(all_rows, w_both, preferred_element_type=jnp.flo...  148 us
    all_gather x1, waiting for transfers between devices, shards(): lax.all_gather(hidden, 'seq', axis=0, tiled=True)  71.9 us
    all_to_all x1, blocking collectives, shards(): lax.all_to_all(jnp.stack(jnp.split(normed, lax.axis_size('seq'), axis=1))...  57.3 us
    reduce_scatter x1, waiting for transfers between devices, shards(): lax.psum_scatter(out_terms.astype(jnp.bfloat16), 'tp', scatter_dimension=...  33.9 us
    dot_general x1, matrix products, shards(): jnp.dot(all_rows, w_both, preferred_element_type=jnp.float32)  21.7 us
    all_to_all x1, blocking collectives, shards(): lax.all_to_all(summed, 'seq', split_axis=0, concat_axis=2, tiled=True)  19.9 us
    dot_general x1, matrix products, shards(): jnp.dot(lax.all_gather(hidden, 'seq', axis=0, tiled=True), down_weight, p...  13.2 us
  transfers between devices with their start and end apart: 4, of which 3 were waited for; matrix products, arithmetic and copies ran while one was open for 0% of the time, Pallas kernels for 0%

profile of v1, /device:TPU:0, one launch (start us, length us, event | category | flops | bytes accessed | tf_op | source)
XLA Modules:
  0.0 393.2 jit_solution(10092200068694339880)
XLA Ops:
  6.5 0.9 slice.34
  7.5 2.4 collective-permute-start
  9.9 1.3 fusion.21
  11.2 2.2 maximum_convert_fusion
  13.4 0.0 copy-start
  13.4 2.2 multiply_reduce_fusion
  15.6 0.0 slice-start
  15.6 0.5 multiply_convert_fusion
  16.2 0.0 slice-start.1
  16.4 57.3 %all_to_all.20 = bf16[8,128,1024]{2,1,0:T(8,128)(2,1)S(1)} all-to-all(bf16[8,128,1024]{2,1,0:T(8,128)(2,1)S(1)} %fusion.11), channel_id=1, replica_groups=mesh['seq'=8,'tp'=4] {'seq'}, dimensions={0} | all-to-all | bytes 4194304 | tf_op jit(solution)/shard_map/all_to_all | solution.py:30
  73.7 21.7 %fusion.4 = bf16[1024,7168]{1,0:T(8,128)(2,1)} fusion(bf16[1024,1024]{1,0:T(8,128)(2,1)S(1)} %bitcast.50, bf16[1024,3584]{1,0:T(8,128)(2,1)S(1)} %bitcast.57, bf16[1024,3584]{1,0:T(8,128)(2,1)} %param.9), kind=kOutput, calls=%fused_computation.4 | convolution fusion | flops 15069085696 | bytes 31457280 | tf_op jit(solution)/shard_map/dot_general | solution.py:36
  95.4 0.0 reduce-scatter.3.cloned.1.call-update
  95.5 0.0 all-gather.2.cloned.1.call-start
  95.5 148.0 %reduce-scatter.3.cloned.1.call-done = bf16[128,7168]{1,0:T(8,128)(2,1)} async-done(((bf16[1024,7168]{1,0:T(8,128)(2,1)}), bf16[128,7168]{1,0:T(8,128)(2,1)}) %reduce-scatter.3.cloned.1.call-update) | async-done | bytes 1835024 | tf_op jit(solution)/shard_map/reduce_scatter | solution.py:35
  243.5 1.9 convert_element_type.24
  245.3 1.4 fusion.10
  246.8 0.0 all-gather.2.cloned.1.call-update
  246.8 0.0 reduce-scatter.5.cloned.1.call-start
  246.9 71.9 %all-gather.2.cloned.1.call-done = bf16[1024,3584]{1,0:T(8,128)(2,1)} async-done(((bf16[128,3584]{1,0:T(8,128)(2,1)}), bf16[1024,3584]{1,0:T(8,128)(2,1)}) %all-gather.2.cloned.1.call-update) | async-done | bytes 7340048 | tf_op jit(solution)/shard_map/all_gather | solution.py:43
  318.8 13.2 %convolution_convert_fusion = bf16[1024,1024]{1,0:T(8,128)(2,1)} fusion(bf16[1024,3584]{1,0:T(8,128)(2,1)} %all-gather.2.cloned.1.call-done, bf16[3584,1024]{1,0:T(8,128)(2,1)} %param.11), kind=kOutput, calls=%fused_computation.15 | convolution fusion | flops 7517241344 | bytes 16777216 | tf_op jit(solution)/shard_map/dot_general | solution.py:42
  332.0 0.0 reduce-scatter.5.cloned.1.call-update
  332.0 33.9 %reduce-scatter.5.cloned.1.call-done = bf16[8,32,1024]{2,1,0:T(8,128)(2,1)} async-done(((bf16[8,128,1024]{2,1,0:T(8,128)(2,1)}), bf16[8,32,1024]{2,1,0:T(8,128)(2,1)}) %reduce-scatter.5.cloned.1.call-update) | async-done | bytes 524304 | tf_op jit(solution)/shard_map/reduce_scatter | solution.py:49
  365.9 19.9 %all_to_all.21 = bf16[8,32,1024]{2,1,0:T(8,128)(2,1)S(1)} all-to-all(bf16[8,32,1024]{2,1,0:T(8,128)(2,1)} %reduce-scatter.5.cloned.1.call-done), channel_id=1, replica_groups=mesh['seq'=8,'tp'=4] {'seq'}, dimensions={0} | all-to-all | bytes 1048576 | tf_op jit(solution)/shard_map/all_to_all | solution.py:50
  385.8 0.8 copy.8
  (15 shorter events, 0.2 us)
Async XLA Ops:
  6.5 237.0 %reduce-scatter.3.cloned.1.call-start = ((), (), s32[]{:S(2)}) async-start(), calls=%async_computation.4 | async-start | bytes 16515072 | tf_op jit(solution)/shard_map/reduce_scatter | solution.py:35
  7.5 3.7 collective-permute-start
  13.4 2.2 copy-start
  15.6 58.1 %slice-start = ((s8[7340032]{0:T(1024)(128)(4,1)}), s8[4194304]{0:T(1024)(128)(4,1)S(1)}, s32[]{:S(2)}) async-start(s8[7340032]{0:T(1024)(128)(4,1)} %bitcast.56), calls=%async_computation.7 | async-start | bytes 8388608
  16.2 57.6 %slice-start.1 = ((s8[7340032]{0:T(1024)(128)(4,1)}), s8[3145728]{0:T(1024)(128)(4,1)S(1)}, s32[]{:S(2)}) async-start(s8[7340032]{0:T(1024)(128)(4,1)} %bitcast.56), calls=%async_computation.8 | async-start | bytes 6291456
  95.5 223.3 %all-gather.2.cloned.1.call-start = ((), (), s32[]{:S(2)}) async-start(), calls=%async_computation.5 | async-start | bytes 8257536 | tf_op jit(solution)/shard_map/all_gather | solution.py:43
  246.8 119.1 %reduce-scatter.5.cloned.1.call-start = ((), (), s32[]{:S(2)}) async-start(), calls=%async_computation.6 | async-start | bytes 2621440 | tf_op jit(solution)/shard_map/reduce_scatter | solution.py:49
Sparse Core Ops, SparseCore 0:
  95.6 147.8 reduce-scatter.2
  246.9 71.8 all-gather.1
  332.1 33.7 reduce-scatter.4
